TPU v7x, 128 devices: a whole 4x4x4 slice. The times are simulated.
128 devices in a mesh: shard: 128 (over y, z, x, core).
Axes of the slice: x: 4, y: 4, z: 4, core: 2. Of those that a mesh axis runs over, the one named last changes fastest.
Arguments:
- lookup_ids: int32 [32768, 4, 8], P('shard'), may hold values from 0 to 524287, as said below
- bag_lengths: int32 [32768, 4], P('shard'), may hold values from 1 to 8
- pooled_gradients: bfloat16 [32768, 4, 128], P('shard'), may hold values from -6 to 6
- tables: float32 [4, 524288, 128], P(None, 'shard'), may hold values from -4 to 4
- accumulators: float32 [4, 524288], P(None, 'shard'), may hold values from 0.05 to 2
Outputs:
- new_tables: float32 [4, 524288, 128], P(None, 'shard')
- new_accumulators: float32 [4, 524288], P(None, 'shard')
- gradient_scale: float32 [], replicated
Inputs may be any that keep to these rules, and one draw needn't show every extreme that they name: `lookup_ids`: row ids are rows 0 to 524287 of their table. Among the 256 x 8 entries of one table held by one device (padding positions included), the rows of every owning device's block of 4096 rows are named exactly 16 times. About half the lookups fall on the first 32 rows of an owner's block.
All inputs are finite; a program needn't handle non-finite values.
Results may differ from a plain program's by a relative error of at most 0.0003.
Values may be sent and summed in bfloat16 or wider, within the bound.
A program may use at most 128 MiB of HBM per device.

v0:
```python
import functools

import jax
import jax.numpy as jnp
from jax import lax
from jax.experimental import pallas as pl
from jax.experimental.pallas import tpu as pltpu
from jax.sharding import PartitionSpec as P

STEP = 0.5
EPS = 1e-08
F32 = jnp.float32
BF16 = jnp.bfloat16
I32 = jnp.int32
MESH = pl.DeviceIdType.MESH
VMEM = pltpu.VMEM


def iota(shape, dim):
    return lax.broadcasted_iota(I32, shape, dim)


def one_if(mask):
    return jnp.where(mask, F32(1.0), F32(0.0)).astype(BF16)


def nt_dot(a, b):
    return lax.dot_general(a, b, (((1,), (1,)), ((), ())), preferred_element_type=F32)


def signal_all(peers):
    me = lax.axis_index("shard")
    barrier = pltpu.get_barrier_semaphore()

    def one(k, carry):
        pl.semaphore_signal(
            barrier, inc=1, device_id=(lax.rem(me + k, peers),), device_id_type=MESH
        )
        return carry

    lax.fori_loop(1, peers, one, 0)
    return barrier


def pack_table(t, ids_ref, len_ref, g32_ref, send_ref, rows32_ref, shift, bucket):
    bags = ids_ref.shape[2]
    width = ids_ref.shape[1]
    peers = send_ref.shape[0]
    lens = len_ref[t : t + 1, :]
    owner_iota = iota((peers, bags), 0)
    bag_iota = iota((1, bags), 1).astype(F32)
    upper = one_if(iota((bags, bags), 0) < iota((bags, bags), 1))
    ones = jnp.ones((bags, bags), BF16)
    prefix_rhs = jnp.concatenate([upper, ones], axis=0)
    rank_iota = iota((bucket, bags), 0).astype(F32)
    seen = jnp.zeros((peers, bags), F32)
    owned = []
    values = []
    for l in range(width):
        ids = ids_ref[t, l : l + 1, :]
        owner = lax.shift_right_logical(ids, shift)
        local = lax.bitwise_and(ids, (1 << shift) - 1)
        own32 = jnp.where(owner == owner_iota, F32(1.0), F32(0.0))
        own = own32.astype(BF16)
        before = jnp.dot(
            jnp.concatenate([own, seen.astype(BF16)], axis=1),
            prefix_rhs,
            preferred_element_type=F32,
        )
        rank = jnp.sum(own32 * before, axis=0, keepdims=True)
        seen = seen + own32
        at_rank = rank == rank_iota
        bag = jnp.where(l < lens, bag_iota, F32(bags))
        high = lax.shift_right_logical(local, 6).astype(F32)
        low = lax.bitwise_and(local, 63).astype(F32)
        zero = jnp.zeros_like(rank_iota)
        values.append(
            jnp.concatenate(
                [
                    jnp.where(at_rank, bag, zero),
                    jnp.where(at_rank, high, zero),
                    jnp.where(at_rank, low, zero),
                ],
                axis=0,
            ).astype(BF16)
        )
        owned.append(own)
    table = nt_dot(jnp.concatenate(owned, axis=1), jnp.concatenate(values, axis=1))
    bag_of = table[:, :bucket]
    rows = (table[:, bucket : 2 * bucket] * 64.0 + table[:, 2 * bucket :]).astype(I32)
    lane = iota((peers, bags), 1).astype(F32)
    select = jnp.concatenate([one_if(bag_of[:, r : r + 1] == lane) for r in range(bucket)], axis=0)
    scaled = g32_ref[t]
    moved = jnp.dot(select, scaled, preferred_element_type=F32)
    for r in range(bucket):
        rows32_ref[pl.ds(r, peers, stride=bucket), :] = moved[r * peers : (r + 1) * peers]
    send_ref[:, t * bucket : (t + 1) * bucket, :] = (
        rows32_ref[...].reshape(peers, bucket, -1).astype(BF16)
    )
    return rows


def exchange_kernel(
    shift,
    bucket,
    ids_ref,
    len_ref,
    g_ref,
    got_ref,
    grow_ref,
    send_ref,
    srow_ref,
    g32_ref,
    scaled_ref,
    rows32_ref,
    send_sem,
    recv_sem,
):
    tables = ids_ref.shape[0]
    bags = ids_ref.shape[2]
    peers = send_ref.shape[0]
    me = lax.axis_index("shard")
    barrier = signal_all(peers)

    g32_ref[...] = g_ref[...].astype(F32)
    lens = len_ref[...].astype(F32)
    lens_t = jnp.concatenate([lens, jnp.ones((128 - tables, bags), F32)], axis=0).T
    for t in range(tables):
        part = g32_ref[pl.ds(t, bags, stride=tables), :]
        scaled_ref[t] = (part / lens_t[:, t : t + 1]).astype(BF16)
    rows = [
        pack_table(t, ids_ref, len_ref, scaled_ref, send_ref, rows32_ref, shift, bucket)
        for t in range(tables)
    ]
    rows.append(jnp.zeros((peers, 128 - tables * bucket), I32))
    srow_ref[...] = jnp.concatenate(rows, axis=1).reshape(srow_ref.shape)

    got_ref[pl.ds(me, 1)] = send_ref[pl.ds(me, 1)]
    grow_ref[pl.ds(me, 1)] = srow_ref[pl.ds(me, 1)]
    pl.semaphore_wait(barrier, peers - 1)

    def send(k, carry):
        p = lax.rem(me + k, peers)
        for i, (src, dst) in enumerate(((srow_ref, grow_ref), (send_ref, got_ref))):
            pltpu.make_async_remote_copy(
                src_ref=src.at[p],
                dst_ref=dst.at[me],
                send_sem=send_sem.at[i],
                recv_sem=recv_sem.at[i],
                device_id=(p,),
                device_id_type=MESH,
            ).start()
        return carry

    lax.fori_loop(1, peers, send, 0)
    others = pl.ds(0, peers - 1)
    for i, (src, dst) in enumerate(((srow_ref, grow_ref), (send_ref, got_ref))):
        pltpu.make_async_copy(dst.at[others], dst.at[others], recv_sem.at[i]).wait()
        pltpu.make_async_copy(src.at[others], src.at[others], send_sem.at[i]).wait()


def update_kernel(
    bucket,
    got_ref,
    grow_ref,
    acc_ref,
    tab_ref,
    out_ref,
    nacc_ref,
    part_ref,
    tab_vm,
    out_vm,
    low_vm,
    hot_vm,
    rhs_vm,
    square_ref,
    in_sem,
    out_sem,
):
    tables, rows, width = tab_ref.shape
    peers = got_ref.shape[0]
    lookups = peers * bucket
    group = 256 // bucket
    chunks = peers // group
    half = rows // 2
    tiles = half // 256
    loads = [
        pltpu.make_async_copy(tab_ref.at[t], tab_vm.at[t], in_sem.at[t]) for t in range(tables)
    ]
    for load in loads:
        load.start()

    got_rows = grow_ref[...].reshape(peers, 128)
    used = tables * bucket
    upper = lax.shift_right_logical(got_rows, half.bit_length() - 1)
    tile = lax.shift_right_logical(lax.bitwise_and(got_rows, half - 1), 8)
    low = lax.bitwise_and(got_rows, 255)
    spread_lane = iota((128, 256 * tables), 1)
    spread = one_if(
        iota((128, 256 * tables), 0)
        == lax.shift_right_logical(spread_lane, 8) * bucket
        + lax.bitwise_and(spread_lane, bucket - 1)
    )
    lane = iota((peers, 256 * tables), 1)
    own_lane = lax.shift_right_logical(
        lax.bitwise_and(lane, 255), bucket.bit_length() - 1
    ) == lax.bitwise_and(iota((peers, 256 * tables), 0), group - 1)

    def lane_vectors(digit):
        wide = jnp.dot(digit.astype(BF16), spread, preferred_element_type=F32)
        wide = jnp.where(own_lane, wide, F32(0.0)).reshape(chunks, group, 256 * tables)
        return jnp.sum(wide, axis=1)

    lows = lane_vectors(low)
    tiles_of = lane_vectors(tile)
    uppers = lane_vectors(upper)
    upper_t = jnp.concatenate(
        [uppers[:, i * 128 : (i + 1) * 128] for i in range(2 * tables)]
        + [jnp.zeros((128 - 2 * tables * chunks, 128), F32)],
        axis=0,
    ).T
    square_ref[...] = jnp.zeros_like(square_ref)
    acc_t = acc_ref[...].T
    lane_id = iota((128, 128), 1)
    sub_id = iota((256, 256), 0).astype(F32)

    stores = []
    for t in range(tables):
        for c in range(chunks):
            col = slice(c * 256, (c + 1) * 256)
            low_vm[:, col] = one_if(lows[c : c + 1, t * 256 : (t + 1) * 256] == sub_id)
            hot_vm[:, col] = jnp.broadcast_to(
                tiles_of[c : c + 1, t * 256 : (t + 1) * 256], (16, 256)
            ).astype(BF16)
            for h in range(2):
                k = 2 * t + h
                is_upper = upper_t[:, k * chunks + c : k * chunks + c + 1]
                src = slice(c * group + h * group // 2, c * group + (h + 1) * group // 2)
                terms = got_ref[src, t * bucket : (t + 1) * bucket, :].reshape(128, width)
                up = jnp.broadcast_to(is_upper, (128, width)).astype(BF16)
                row = slice(c * 256 + h * 128, c * 256 + (h + 1) * 128)
                rhs_vm[row, width:] = terms * up
                rhs_vm[row, :width] = terms * (BF16(1.0) - up)
        loads[t].wait()

        def tile_step(m, carry, t=t):
            mask = jnp.where(
                hot_vm[...] == m.astype(F32).astype(BF16), BF16(1.0), BF16(0.0)
            )
            lhs = (low_vm[...].reshape(16, 16, lookups) * mask[None]).reshape(256, lookups)
            both = jnp.dot(lhs, rhs_vm[...], preferred_element_type=F32)
            for p in range(2):
                for h in range(2):
                    s = both[h * 128 : (h + 1) * 128, p * width : (p + 1) * width]
                    block = p * (half // 128) + 2 * m + h
                    out_vm[t, pl.ds(pl.multiple_of(block * 128, 128), 128), :] = s
                    squares = jnp.sum(s * s, axis=1, keepdims=True)
                    square_ref[...] = jnp.where(
                        lane_id == block * tables + t, squares, square_ref[...]
                    )
            return carry

        lax.fori_loop(0, tiles, tile_step, 0)
        new_acc = acc_t + square_ref[...] * F32(1.0 / width)
        rate = STEP / (jnp.sqrt(new_acc) + EPS)
        for block in range(rows // 128):
            at = slice(block * 128, (block + 1) * 128)
            lane_at = block * tables + t
            out_vm[t, at, :] = tab_vm[t, at, :] - out_vm[t, at, :] * rate[:, lane_at : lane_at + 1]
        store = pltpu.make_async_copy(out_vm.at[t], out_ref.at[t], out_sem.at[t])
        store.start()
        stores.append(store)
    nacc_ref[...] = (acc_t + square_ref[...] * F32(1.0 / width)).T
    part_ref[...] = jnp.broadcast_to(
        jnp.sum(jnp.sum(square_ref[...], axis=1, keepdims=True), axis=0, keepdims=True), (8, 128)
    )
    for store in stores:
        store.wait()


def total_kernel(count, part_ref, out_ref, got_ref, send_sem, recv_sem):
    peers = got_ref.shape[0]
    me = lax.axis_index("shard")
    barrier = signal_all(peers)
    got_ref[pl.ds(me, 1)] = part_ref[0:1].reshape(1, 1, 128)
    pl.semaphore_wait(barrier, peers - 1)

    def send(k, carry):
        p = lax.rem(me + k, peers)
        pltpu.make_async_remote_copy(
            src_ref=part_ref.at[pl.ds(0, 1)],
            dst_ref=got_ref.at[me],
            send_sem=send_sem,
            recv_sem=recv_sem,
            device_id=(p,),
            device_id_type=MESH,
        ).start()
        return carry

    lax.fori_loop(1, peers, send, 0)
    others = pl.ds(0, peers - 1)
    pltpu.make_async_copy(got_ref.at[others], got_ref.at[others], recv_sem).wait()
    pltpu.make_async_copy(got_ref.at[others], got_ref.at[others], send_sem).wait()
    total = jnp.sum(got_ref[...].reshape(peers, 128), axis=0, keepdims=True)
    out_ref[...] = jnp.broadcast_to(jnp.sqrt(total * F32(1.0 / count)), out_ref.shape)


def per_device(peers, lookup_ids, bag_lengths, pooled_gradients, tables, accumulators):
    samples, count_tables, bag_width = lookup_ids.shape
    width = pooled_gradients.shape[2]
    rows_dev = tables.shape[1]
    lookups = samples * bag_width
    bucket = lookups // peers
    blocks = rows_dev // 128
    in_vmem = pl.BlockSpec(memory_space=VMEM)
    in_any = pl.BlockSpec(memory_space=pl.ANY)
    got, got_rows = pl.pallas_call(
        functools.partial(exchange_kernel, rows_dev.bit_length() - 1, bucket),
        out_shape=(
            jax.ShapeDtypeStruct((peers, count_tables * bucket, width), BF16),
            jax.ShapeDtypeStruct((peers, 1, 128), I32),
        ),
        in_specs=[in_vmem] * 3,
        out_specs=(in_vmem, in_vmem),
        scratch_shapes=[
            VMEM((peers, count_tables * bucket, width), BF16),
            VMEM((peers, 1, 128), I32),
            VMEM((samples * count_tables, width), F32),
            VMEM((count_tables, samples, width), BF16),
            VMEM((peers * bucket, width), F32),
            pltpu.SemaphoreType.DMA((2,)),
            pltpu.SemaphoreType.DMA((2,)),
        ],
        compiler_params=pltpu.CompilerParams(collective_id=0, has_side_effects=True),
        name="exchange",
    )(
        lookup_ids.transpose(1, 2, 0),
        bag_lengths.T,
        pooled_gradients.reshape(samples * count_tables, width),
    )
    acc = accumulators.reshape(count_tables, blocks, 128).transpose(1, 0, 2).reshape(-1, 128)
    new_tables, new_acc, part = pl.pallas_call(
        functools.partial(update_kernel, bucket),
        out_shape=(
            jax.ShapeDtypeStruct(tables.shape, F32),
            jax.ShapeDtypeStruct(acc.shape, F32),
            jax.ShapeDtypeStruct((8, 128), F32),
        ),
        in_specs=[in_vmem] * 3 + [in_any],
        out_specs=(in_any, in_vmem, in_vmem),
        scratch_shapes=[
            VMEM(tables.shape, F32),
            VMEM(tables.shape, F32),
            VMEM((256, lookups), BF16),
            VMEM((16, lookups), BF16),
            VMEM((lookups, 2 * width), BF16),
            VMEM((128, 128), F32),
            pltpu.SemaphoreType.DMA((count_tables,)),
            pltpu.SemaphoreType.DMA((count_tables,)),
        ],
        name="update",
    )(got, got_rows, acc, tables)
    new_acc = new_acc.reshape(blocks, count_tables, 128).transpose(1, 0, 2).reshape(accumulators.shape)
    count = width * count_tables * lookups * peers
    total = pl.pallas_call(
        functools.partial(total_kernel, count),
        out_shape=jax.ShapeDtypeStruct((8, 128), F32),
        in_specs=[in_vmem],
        out_specs=in_vmem,
        scratch_shapes=[
            VMEM((peers, 1, 128), F32),
            pltpu.SemaphoreType.DMA,
            pltpu.SemaphoreType.DMA,
        ],
        compiler_params=pltpu.CompilerParams(collective_id=1, has_side_effects=True),
        name="total",
    )(part)
    return (new_tables, new_acc, total[0, 0])


def solution(mesh):
    peers = mesh.devices.size
    return jax.shard_map(
        functools.partial(per_device, peers),
        mesh=mesh,
        in_specs=(
            P("shard", None, None),
            P("shard", None),
            P("shard", None, None),
            P(None, "shard", None),
            P(None, "shard"),
        ),
        out_specs=(P(None, "shard", None), P(None, "shard"), P()),
        check_vma=False,
    )
```

profile of v0, /device:TPU:1, one launch (start us, length us, event | category | flops | bytes accessed | tf_op | source)
XLA Modules:
  0.0 91.5 jit_solution(5060028499719121603)
XLA Ops:
  0.6 48.9 %exchange.1 = (bf16[128,64,128]{2,1,0:T(8,128)(2,1)}, s32[128,1,128]{2,1,0:T(1,128)}) custom-call(s32[4,8,256]{2,1,0:T(8,128)} %bitcast.16, s32[4,256]{1,0:T(4,128)} %bitcast.17, bf16[1024,128]{1,0:T(8,128)(2,1)} %bitcast.14), custom_call_target="tpu_custom_call" | custom-call | tf_op jit(solution)/shard_map/exchange/pallas_call | solution.py:317
  49.5 26.1 %update.1 = (f32[4,4096,128]{2,1,0:T(8,128)}, f32[128,128]{1,0:T(8,128)}, f32[8,128]{1,0:T(8,128)}) custom-call(bf16[128,64,128]{2,1,0:T(8,128)(2,1)} %get-tuple-element.8.got_ref, s32[128,1,128]{2,1,0:T(1,128)} %get-tuple-element.9.grow_ref, f32[128,128]{1,0:T(8,128)} %bitcast.15, f32[4,4096,128]{2,1,0:T(8,128)} %tab_ref.1), custom_call_target="tpu_custom_call" | custom-call | tf_op jit(solution)/shard_map/update/pallas_call | solution.py:342
  75.7 14.6 %total.1 = f32[8,128]{1,0:T(8,128)} custom-call(f32[8,128]{1,0:T(8,128)} %get-tuple-element.12.part_ref), custom_call_target="tpu_custom_call" | custom-call | tf_op jit(solution)/shard_map/total/pallas_call | solution.py:365
  90.3 1.2 %slice.3 = f32[1,1]{1,0:T(1,128)} slice(f32[8,128]{1,0:T(8,128)} %total.1), slice={[0:1], [0:1]} | slice | bytes 8 | tf_op jit(solution)/shard_map/slice | solution.py:378
where the time goes:
time: 91.7 us; the launch traced here: 91.5 us
  Pallas kernels  89.6 us (98%)
  local copies, waits for them, and re-layouts  1.18 us (1%)
    pallas_call x1, Pallas kernels, per_device(): pl.pallas_call(functools.partial(exchange_kernel, rows_dev.bit_length() -...  48.9 us
    pallas_call x1, Pallas kernels, per_device(): pl.pallas_call(functools.partial(update_kernel, bucket), out_shape=(jax.S...  26.1 us
    pallas_call x1, Pallas kernels, per_device(): pl.pallas_call(functools.partial(total_kernel, count), out_shape=jax.Shap...  14.6 us

commit v1 on v0

v1 whole, which is shorter than its diff:
```python
import functools

import jax
import jax.numpy as jnp
from jax import lax
from jax.experimental import pallas as pl
from jax.experimental.pallas import tpu as pltpu
from jax.sharding import PartitionSpec as P

STEP = 0.5
EPS = 1e-08
F32 = jnp.float32
BF16 = jnp.bfloat16
I32 = jnp.int32
MESH = pl.DeviceIdType.MESH
VMEM = pltpu.VMEM


def iota(shape, dim):
    return lax.broadcasted_iota(I32, shape, dim)


def one_if(mask):
    return jnp.where(mask, F32(1.0), F32(0.0)).astype(BF16)


def nt_dot(a, b):
    return lax.dot_general(a, b, (((1,), (1,)), ((), ())), preferred_element_type=F32)


def signal_all(peers):
    me = lax.axis_index("shard")
    barrier = pltpu.get_barrier_semaphore()

    def one(k, carry):
        pl.semaphore_signal(
            barrier, inc=1, device_id=(lax.rem(me + k, peers),), device_id_type=MESH
        )
        return carry

    lax.fori_loop(1, peers, one, 0)
    return barrier


def rank_table(t, ids_ref, len_ref, peers, shift, bucket):
    bags = ids_ref.shape[2]
    width = ids_ref.shape[1]
    lens = len_ref[t : t + 1, :]
    owner_iota = iota((peers, bags), 0)
    bag_iota = iota((1, bags), 1).astype(F32)
    upper = one_if(iota((bags, bags), 0) < iota((bags, bags), 1))
    ones = jnp.ones((bags, bags), BF16)
    prefix_rhs = jnp.concatenate([upper, ones], axis=0)
    rank_iota = iota((bucket, bags), 0).astype(F32)
    seen = jnp.zeros((peers, bags), F32)
    owned = []
    values = []
    for l in range(width):
        ids = ids_ref[t, l : l + 1, :]
        owner = lax.shift_right_logical(ids, shift)
        local = lax.bitwise_and(ids, (1 << shift) - 1)
        own32 = jnp.where(owner == owner_iota, F32(1.0), F32(0.0))
        own = own32.astype(BF16)
        before = jnp.dot(
            jnp.concatenate([own, seen.astype(BF16)], axis=1),
            prefix_rhs,
            preferred_element_type=F32,
        )
        rank = jnp.sum(own32 * before, axis=0, keepdims=True)
        seen = seen + own32
        at_rank = rank == rank_iota
        bag = jnp.where(l < lens, bag_iota, F32(bags))
        high = lax.shift_right_logical(local, 6).astype(F32)
        low = lax.bitwise_and(local, 63).astype(F32)
        zero = jnp.zeros_like(rank_iota)
        values.append(
            jnp.concatenate(
                [
                    jnp.where(at_rank, bag, zero),
                    jnp.where(at_rank, high, zero),
                    jnp.where(at_rank, low, zero),
                ],
                axis=0,
            ).astype(BF16)
        )
        owned.append(own)
    table = nt_dot(jnp.concatenate(owned, axis=1), jnp.concatenate(values, axis=1))
    rows = (table[:, bucket : 2 * bucket] * 64.0 + table[:, 2 * bucket :]).astype(I32)
    return table[:, :bucket], rows


def select_table(t, bag_of, scaled_ref, send_ref, rows32_ref):
    peers, bucket = bag_of.shape
    bags = scaled_ref.shape[1]
    lane = iota((peers, bags), 1).astype(F32)
    select = jnp.concatenate([one_if(bag_of[:, r : r + 1] == lane) for r in range(bucket)], axis=0)
    moved = jnp.dot(select, scaled_ref[t], preferred_element_type=F32)
    for r in range(bucket):
        rows32_ref[pl.ds(r, peers, stride=bucket), :] = moved[r * peers : (r + 1) * peers]
    send_ref[t] = rows32_ref[...].reshape(peers, bucket, -1).astype(BF16)


def exchange_and_update(
    sizes,
    stride,
    shift,
    bucket,
    count,
    ids_hbm,
    len_hbm,
    g_hbm,
    acc_hbm,
    tab_ref,
    out_ref,
    nacc_ref,
    scale_ref,
    ids_ref,
    len_ref,
    g_ref,
    acc_ref,
    send_ref,
    srow_ref,
    got_ref,
    grow_ref,
    g32_ref,
    scaled_ref,
    rows32_ref,
    sum_ref,
    low_ref,
    hot_ref,
    rhs_ref,
    square_ref,
    part_ref,
    parts_ref,
    in_sem,
    send_sem,
    recv_sem,
):
    tables, rows, width = tab_ref.shape
    bags = ids_ref.shape[2]
    peers = send_ref.shape[1]
    lookups = peers * bucket
    group = 256 // bucket
    chunks = peers // group
    half = rows // 2
    tiles = half // 256
    me = lax.axis_index("shard")
    loads = [
        pltpu.make_async_copy(tab_ref.at[t], out_ref.at[t], in_sem.at[t]) for t in range(tables)
    ]
    small = [
        pltpu.make_async_copy(src, dst, in_sem.at[tables + i])
        for i, (src, dst) in enumerate(
            ((ids_hbm, ids_ref), (len_hbm, len_ref), (g_hbm, g_ref), (acc_hbm, acc_ref))
        )
    ]
    for load in small + loads:
        load.start()
    barrier = signal_all(peers)
    for load in small:
        load.wait()

    g32_ref[...] = g_ref[...].astype(F32)
    lens = len_ref[...].astype(F32)
    lens_t = jnp.concatenate([lens, jnp.ones((128 - tables, bags), F32)], axis=0).T
    for t in range(tables):
        part = g32_ref[pl.ds(t, bags, stride=tables), :]
        scaled_ref[t] = (part / lens_t[:, t : t + 1]).astype(BF16)
    ranked = [rank_table(t, ids_ref, len_ref, peers, shift, bucket) for t in range(tables)]
    srow_ref[...] = jnp.concatenate(
        [r for _, r in ranked] + [jnp.zeros((peers, 128 - tables * bucket), I32)], axis=1
    ).reshape(srow_ref.shape)

    near = []
    span = peers
    for size in sizes:
        span //= size
        here = lax.rem(lax.div(me, span), size)
        near.append([lax.rem(here + d, size) * span for d in range(size)])

    def peer_at(slot):
        offset = (stride * slot) % (peers - 1) + 1
        span = peers
        where = None
        for size, spots in zip(sizes, near):
            span //= size
            spot = spots[offset // span % size]
            where = spot if where is None else where + spot
        return where

    def send_all(src, dst, s):
        for slot in range(peers - 1):
            p = peer_at(slot)
            pltpu.make_async_remote_copy(
                src_ref=src(p),
                dst_ref=dst(slot),
                send_sem=send_sem.at[s],
                recv_sem=recv_sem.at[s],
                device_id=(p,),
                device_id_type=MESH,
            ).start()

    def send_table(t):
        send_all(lambda p: send_ref.at[t, p], lambda slot: got_ref.at[t, slot], t)

    others = pl.ds(0, peers - 1)

    select_table(0, ranked[0][0], scaled_ref, send_ref, rows32_ref)
    select_table(1, ranked[1][0], scaled_ref, send_ref, rows32_ref)
    pl.semaphore_wait(barrier, peers - 1)
    send_all(lambda p: srow_ref.at[p], lambda slot: grow_ref.at[slot], tables)
    send_table(0)
    for t in range(2, tables):
        select_table(t, ranked[t][0], scaled_ref, send_ref, rows32_ref)
        send_table(t - 1)
    grow_ref[pl.ds(peers - 1, 1)] = srow_ref[pl.ds(me, 1)]
    for t in range(tables):
        got_ref[t, pl.ds(peers - 1, 1)] = send_ref[t, pl.ds(me, 1)]
    send_table(tables - 1)
    acc_t = acc_ref[...].T
    square_ref[...] = jnp.zeros_like(square_ref)

    pltpu.make_async_copy(
        grow_ref.at[others], grow_ref.at[others], recv_sem.at[tables]
    ).wait()
    got_rows = grow_ref[...].reshape(peers, 128)
    upper = lax.shift_right_logical(got_rows, half.bit_length() - 1)
    tile = lax.shift_right_logical(lax.bitwise_and(got_rows, half - 1), 8)
    low = lax.bitwise_and(got_rows, 255)
    spread_lane = iota((128, 256 * tables), 1)
    spread = one_if(
        iota((128, 256 * tables), 0)
        == lax.shift_right_logical(spread_lane, 8) * bucket
        + lax.bitwise_and(spread_lane, bucket - 1)
    )
    lane = iota((peers, 256 * tables), 1)
    own_lane = lax.shift_right_logical(
        lax.bitwise_and(lane, 255), bucket.bit_length() - 1
    ) == lax.bitwise_and(iota((peers, 256 * tables), 0), group - 1)

    def lane_vectors(digit):
        wide = jnp.dot(digit.astype(BF16), spread, preferred_element_type=F32)
        wide = jnp.where(own_lane, wide, F32(0.0)).reshape(chunks, group, 256 * tables)
        return jnp.sum(wide, axis=1)

    lows = lane_vectors(low)
    tiles_of = lane_vectors(tile)
    uppers = lane_vectors(upper)
    upper_t = jnp.concatenate(
        [uppers[:, i * 128 : (i + 1) * 128] for i in range(2 * tables)]
        + [jnp.zeros((128 - 2 * tables * chunks, 128), F32)],
        axis=0,
    ).T
    lane_id = iota((128, 128), 1)
    sub_id = iota((256, 256), 0).astype(F32)

    for t in range(tables):
        for c in range(chunks):
            col = slice(c * 256, (c + 1) * 256)
            low_ref[:, col] = one_if(lows[c : c + 1, t * 256 : (t + 1) * 256] == sub_id)
            hot_ref[:, col] = jnp.broadcast_to(
                tiles_of[c : c + 1, t * 256 : (t + 1) * 256], (16, 256)
            ).astype(BF16)
        pltpu.make_async_copy(
            got_ref.at[t, others], got_ref.at[t, others], recv_sem.at[t]
        ).wait()
        for c in range(chunks):
            for h in range(2):
                k = 2 * t + h
                is_upper = upper_t[:, k * chunks + c : k * chunks + c + 1]
                src = slice(c * group + h * group // 2, c * group + (h + 1) * group // 2)
                terms = got_ref[t, src].reshape(128, width)
                up = jnp.broadcast_to(is_upper, (128, width)).astype(BF16)
                row = slice(c * 256 + h * 128, c * 256 + (h + 1) * 128)
                rhs_ref[row, width:] = terms * up
                rhs_ref[row, :width] = terms * (BF16(1.0) - up)

        def tile_step(m, carry, t=t):
            mask = jnp.where(hot_ref[...] == m.astype(F32).astype(BF16), BF16(1.0), BF16(0.0))
            lhs = (low_ref[...].reshape(16, 16, lookups) * mask[None]).reshape(256, lookups)
            both = jnp.dot(lhs, rhs_ref[...], preferred_element_type=F32)
            for p in range(2):
                for h in range(2):
                    s = both[h * 128 : (h + 1) * 128, p * width : (p + 1) * width]
                    block = p * (half // 128) + 2 * m + h
                    sum_ref[pl.ds(pl.multiple_of(block * 128, 128), 128), :] = s
                    squares = jnp.sum(s * s, axis=1, keepdims=True)
                    square_ref[...] = jnp.where(
                        lane_id == block * tables + t, squares, square_ref[...]
                    )
            return carry

        lax.fori_loop(0, tiles, tile_step, 0)
        if t == tables - 1:
            part_ref[...] = jnp.broadcast_to(
                jnp.sum(square_ref[...], axis=0, keepdims=True), part_ref.shape
            )
        new_acc = acc_t + square_ref[...] * F32(1.0 / width)
        rate = STEP / (jnp.sqrt(new_acc) + EPS)
        loads[t].wait()
        for block in range(rows // 128):
            at = slice(block * 128, (block + 1) * 128)
            lane_at = block * tables + t
            out_ref[t, at, :] = out_ref[t, at, :] - sum_ref[at, :] * rate[:, lane_at : lane_at + 1]
            if t == tables - 1 and block == 3:
                send_all(
                    lambda p: part_ref.at[pl.ds(0, 1)],
                    lambda slot: parts_ref.at[slot],
                    tables + 1,
                )
    nacc_ref[...] = (acc_t + square_ref[...] * F32(1.0 / width)).T
    parts_ref[pl.ds(peers - 1, 1)] = part_ref[0:1].reshape(1, 1, 128)
    pltpu.make_async_copy(
        parts_ref.at[others], parts_ref.at[others], recv_sem.at[tables + 1]
    ).wait()
    total = jnp.sum(parts_ref[...].reshape(peers, 128), axis=0, keepdims=True)
    total = jnp.sum(total, axis=1, keepdims=True)
    scale_ref[...] = jnp.broadcast_to(jnp.sqrt(total * F32(1.0 / count)), scale_ref.shape)
    for t in range(tables):
        pltpu.make_async_copy(
            send_ref.at[t, others], send_ref.at[t, others], send_sem.at[t]
        ).wait()
    pltpu.make_async_copy(
        srow_ref.at[others], srow_ref.at[others], send_sem.at[tables]
    ).wait()
    pltpu.make_async_copy(
        parts_ref.at[others], parts_ref.at[others], send_sem.at[tables + 1]
    ).wait()


def write_out(tab_ref, acc_ref, scale_ref, out_ref, nacc_ref, total_ref, sem):
    tables = tab_ref.shape[0]
    stores = [
        pltpu.make_async_copy(tab_ref.at[t], out_ref.at[t], sem.at[t]) for t in range(tables)
    ]
    for store in stores:
        store.start()
    nacc_ref[...] = acc_ref[...]
    total_ref[...] = scale_ref[0:1, 0:1]
    for store in stores:
        store.wait()


def per_device(peers, sizes, lookup_ids, bag_lengths, pooled_gradients, tables, accumulators):
    samples, count_tables, bag_width = lookup_ids.shape
    width = pooled_gradients.shape[2]
    rows_dev = tables.shape[1]
    lookups = samples * bag_width
    bucket = lookups // peers
    blocks = rows_dev // 128
    count = width * count_tables * lookups * peers
    in_vmem = pl.BlockSpec(memory_space=VMEM)
    in_any = pl.BlockSpec(memory_space=pl.ANY)
    in_hbm = pl.BlockSpec(memory_space=pltpu.HBM)
    acc = accumulators.reshape(count_tables, blocks, 128).transpose(1, 0, 2).reshape(-1, 128)
    moved, new_acc, scale = pl.pallas_call(
        functools.partial(
            exchange_and_update, sizes, 37, rows_dev.bit_length() - 1, bucket, count
        ),
        out_shape=(
            VMEM(tables.shape, F32),
            VMEM(acc.shape, F32),
            VMEM((8, 128), F32),
        ),
        in_specs=[in_hbm] * 5,
        out_specs=(in_vmem, in_vmem, in_vmem),
        scratch_shapes=[
            VMEM((count_tables, bag_width, samples), I32),
            VMEM((count_tables, samples), I32),
            VMEM((samples * count_tables, width), BF16),
            VMEM(acc.shape, F32),
            VMEM((count_tables, peers, bucket, width), BF16),
            VMEM((peers, 1, 128), I32),
            VMEM((count_tables, peers, bucket, width), BF16),
            VMEM((peers, 1, 128), I32),
            VMEM((samples * count_tables, width), F32),
            VMEM((count_tables, samples, width), BF16),
            VMEM((peers * bucket, width), F32),
            VMEM((rows_dev, width), F32),
            VMEM((256, lookups), BF16),
            VMEM((16, lookups), BF16),
            VMEM((lookups, 2 * width), BF16),
            VMEM((128, 128), F32),
            VMEM((8, 128), F32),
            VMEM((peers, 1, 128), F32),
            pltpu.SemaphoreType.DMA((count_tables + 4,)),
            pltpu.SemaphoreType.DMA((count_tables + 2,)),
            pltpu.SemaphoreType.DMA((count_tables + 2,)),
        ],
        compiler_params=pltpu.CompilerParams(
            collective_id=0, has_side_effects=True, vmem_limit_bytes=58_585_088
        ),
        name="exchange",
    )(
        lookup_ids.transpose(1, 2, 0),
        bag_lengths.T,
        pooled_gradients.reshape(samples * count_tables, width),
        acc,
        tables,
    )
    new_tables, new_acc, total = pl.pallas_call(
        write_out,
        out_shape=(
            jax.ShapeDtypeStruct(tables.shape, F32),
            jax.ShapeDtypeStruct(acc.shape, F32),
            jax.ShapeDtypeStruct((1, 1), F32),
        ),
        in_specs=[in_vmem] * 3,
        out_specs=(in_any, in_vmem, in_vmem),
        scratch_shapes=[pltpu.SemaphoreType.DMA((count_tables,))],
        compiler_params=pltpu.CompilerParams(vmem_limit_bytes=16 * 2**20),
        name="write_out",
    )(moved, new_acc, scale)
    new_acc = new_acc.reshape(blocks, count_tables, 128).transpose(1, 0, 2).reshape(accumulators.shape)
    return (new_tables, new_acc, total[0, 0])


def solution(mesh):
    peers = mesh.devices.size
    return jax.shard_map(
        functools.partial(per_device, peers, (4, 4, 4, 2)),
        mesh=mesh,
        in_specs=(
            P("shard", None, None),
            P("shard", None),
            P("shard", None, None),
            P(None, "shard", None),
            P(None, "shard"),
        ),
        out_specs=(P(None, "shard", None), P(None, "shard"), P()),
        check_vma=False,
    )
```

time: 91.7 us -> 55.9 us (0.61)
  Pallas kernels: 89.6 us -> 55 us
  local copies, waits for them, and re-layouts: 1.18 us -> 0 us
    pallas_call x3 -> x2, Pallas kernels: 89.6 us -> 55 us  [the longest x1 51 us: per_device(): pl.pallas_call(functools.partial(exchange_and_update, sizes, 37, rows_dev...]
    slice x1 -> x0, local copies, waits for them, and re-layouts: 1.18 us -> none  [per_device(): return (new_tables, new_acc, total[0, 0])]
where the time goes in v1:
time: 55.9 us; the launch traced here: 55.8 us
  Pallas kernels  55 us (98%)
  between operations  0.8 us (1%)
    pallas_call x1, Pallas kernels, per_device(): pl.pallas_call(functools.partial(exchange_and_update, sizes, 37, rows_dev...  51 us
    pallas_call x1, Pallas kernels, per_device(): pl.pallas_call(write_out, out_shape=(jax.ShapeDtypeStruct(tables.shape, F...  4 us

profile of v1, /device:TPU:1, one launch (start us, length us, event | category | flops | bytes accessed | tf_op | source)
XLA Modules:
  0.0 55.8 jit_solution(3264283052176105483)
XLA Ops:
  0.6 51.0 %exchange.1 = (f32[4,4096,128]{2,1,0:T(8,128)S(1)}, f32[128,128]{1,0:T(8,128)S(1)}, f32[8,128]{1,0:T(8,128)S(1)}) custom-call(s32[4,8,256]{2,1,0:T(8,128)} %bitcast.16, s32[4,256]{1,0:T(4,128)} %bitcast.17, bf16[1024,128]{1,0:T(8,128)(2,1)} %bitcast.14, f32[128,128]{1,0:T(8,128)} %bitcast.15, f32[4,4096,128]{2,1,0:T(8,128)} %tab_ref.1), custom_call_target="tpu_custom_call" | custom-call | tf_op jit(solution)/shard_map/exchange/pallas_call | solution.py:356
  51.7 4.0 %write_out.1 = (f32[4,4096,128]{2,1,0:T(8,128)}, f32[128,128]{1,0:T(8,128)}, f32[1,1]{1,0:T(1,128)}) custom-call(f32[4,4096,128]{2,1,0:T(8,128)S(1)} %get-tuple-element.9.tab_ref, f32[128,128]{1,0:T(8,128)S(1)} %get-tuple-element.10.acc_ref, f32[8,128]{1,0:T(8,128)S(1)} %get-tuple-element.11.scale_ref), custom_call_target="tpu_custom_call" | custom-call | tf_op jit(solution)/shard_map/write_out/pallas_call | solution.py:401

commit v2 on v1

--- a/solution.py
+++ b/solution.py
@@ -28,18 +28,24 @@
     return lax.dot_general(a, b, (((1,), (1,)), ((), ())), preferred_element_type=F32)
 
 
-def signal_all(peers):
-    me = lax.axis_index("shard")
-    barrier = pltpu.get_barrier_semaphore()
-
-    def one(k, carry):
-        pl.semaphore_signal(
-            barrier, inc=1, device_id=(lax.rem(me + k, peers),), device_id_type=MESH
-        )
-        return carry
-
-    lax.fori_loop(1, peers, one, 0)
-    return barrier
+def send_order(sizes):
+    peers = 1
+    for size in sizes:
+        peers *= size
+    even = []
+    for k in range(peers - 1):
+        rest = (37 * k) % (peers - 1) + 1
+        offset = []
+        for size in reversed(sizes):
+            offset.insert(0, rest % size)
+            rest //= size
+        even.append(tuple(offset))
+
+    def hops(offset):
+        return sum(min(d, size - d) for d, size in zip(offset[:-1], sizes))
+
+    far = sorted(even, key=lambda offset: -hops(offset))
+    return far, [far.index(offset) for offset in even]
 
 
 def rank_table(t, ids_ref, len_ref, peers, shift, bucket):
@@ -102,7 +108,6 @@
 
 def exchange_and_update(
     sizes,
-    stride,
     shift,
     bucket,
     count,
@@ -156,7 +161,20 @@
     ]
     for load in small + loads:
         load.start()
-    barrier = signal_all(peers)
+    near = []
+    span = peers
+    for size in sizes:
+        span //= size
+        here = lax.rem(lax.div(me, span), size)
+        near.append([lax.rem(here + d, size) * span for d in range(size)])
+    far, even = send_order(sizes)
+
+    def peer_at(slot):
+        return sum(spots[d] for spots, d in zip(near, far[slot]))
+
+    barrier = pltpu.get_barrier_semaphore()
+    for slot in range(peers - 1):
+        pl.semaphore_signal(barrier, inc=1, device_id=(peer_at(slot),), device_id_type=MESH)
     for load in small:
         load.wait()
 
@@ -171,25 +189,8 @@
         [r for _, r in ranked] + [jnp.zeros((peers, 128 - tables * bucket), I32)], axis=1
     ).reshape(srow_ref.shape)
 
-    near = []
-    span = peers
-    for size in sizes:
-        span //= size
-        here = lax.rem(lax.div(me, span), size)
-        near.append([lax.rem(here + d, size) * span for d in range(size)])
-
-    def peer_at(slot):
-        offset = (stride * slot) % (peers - 1) + 1
-        span = peers
-        where = None
-        for size, spots in zip(sizes, near):
-            span //= size
-            spot = spots[offset // span % size]
-            where = spot if where is None else where + spot
-        return where
-
-    def send_all(src, dst, s):
-        for slot in range(peers - 1):
+    def send_all(src, dst, s, slots=range(peers - 1)):
+        for slot in slots:
             p = peer_at(slot)
             pltpu.make_async_remote_copy(
                 src_ref=src(p),
@@ -200,16 +201,35 @@
                 device_id_type=MESH,
             ).start()
 
+    last = tables - 1
+    rows_sem = tables
+    parts_sem = tables + 1
+    tail = [(0, chunks // 2), (chunks // 2, 3 * chunks // 4), (3 * chunks // 4, chunks)]
+    tail_sems = [last, tables + 2, tables + 3]
+
     def send_table(t):
-        send_all(lambda p: send_ref.at[t, p], lambda slot: got_ref.at[t, slot], t)
-
-    others = pl.ds(0, peers - 1)
+        def src(p):
+            return send_ref.at[t, p]
+
+        def dst(slot):
+            return got_ref.at[t, slot]
+
+        if t < last:
+            send_all(src, dst, t, even)
+        else:
+            for (c0, c1), s in zip(tail, tail_sems):
+                send_all(src, dst, s, range(c0 * group, min(c1 * group, peers - 1)))
+
+    def wait_for(ref, s, begin, end):
+        part = ref.at[pl.ds(begin, end - begin)]
+        pltpu.make_async_copy(part, part, s).wait()
+
 
     select_table(0, ranked[0][0], scaled_ref, send_ref, rows32_ref)
     select_table(1, ranked[1][0], scaled_ref, send_ref, rows32_ref)
     pl.semaphore_wait(barrier, peers - 1)
-    send_all(lambda p: srow_ref.at[p], lambda slot: grow_ref.at[slot], tables)
     send_table(0)
+    send_all(lambda p: srow_ref.at[p], lambda slot: grow_ref.at[slot], rows_sem, even)
     for t in range(2, tables):
         select_table(t, ranked[t][0], scaled_ref, send_ref, rows32_ref)
         send_table(t - 1)
@@ -220,9 +240,7 @@
     acc_t = acc_ref[...].T
     square_ref[...] = jnp.zeros_like(square_ref)
 
-    pltpu.make_async_copy(
-        grow_ref.at[others], grow_ref.at[others], recv_sem.at[tables]
-    ).wait()
+    wait_for(grow_ref, recv_sem.at[rows_sem], 0, peers - 1)
     got_rows = grow_ref[...].reshape(peers, 128)
     upper = lax.shift_right_logical(got_rows, half.bit_length() - 1)
     tile = lax.shift_right_logical(lax.bitwise_and(got_rows, half - 1), 8)
@@ -261,36 +279,50 @@
             hot_ref[:, col] = jnp.broadcast_to(
                 tiles_of[c : c + 1, t * 256 : (t + 1) * 256], (16, 256)
             ).astype(BF16)
-        pltpu.make_async_copy(
-            got_ref.at[t, others], got_ref.at[t, others], recv_sem.at[t]
-        ).wait()
-        for c in range(chunks):
-            for h in range(2):
-                k = 2 * t + h
-                is_upper = upper_t[:, k * chunks + c : k * chunks + c + 1]
-                src = slice(c * group + h * group // 2, c * group + (h + 1) * group // 2)
-                terms = got_ref[t, src].reshape(128, width)
-                up = jnp.broadcast_to(is_upper, (128, width)).astype(BF16)
-                row = slice(c * 256 + h * 128, c * 256 + (h + 1) * 128)
-                rhs_ref[row, width:] = terms * up
-                rhs_ref[row, :width] = terms * (BF16(1.0) - up)
-
-        def tile_step(m, carry, t=t):
-            mask = jnp.where(hot_ref[...] == m.astype(F32).astype(BF16), BF16(1.0), BF16(0.0))
-            lhs = (low_ref[...].reshape(16, 16, lookups) * mask[None]).reshape(256, lookups)
-            both = jnp.dot(lhs, rhs_ref[...], preferred_element_type=F32)
-            for p in range(2):
+
+        def add_chunks(c0, c1, t=t):
+            for c in range(c0, c1):
                 for h in range(2):
-                    s = both[h * 128 : (h + 1) * 128, p * width : (p + 1) * width]
-                    block = p * (half // 128) + 2 * m + h
-                    sum_ref[pl.ds(pl.multiple_of(block * 128, 128), 128), :] = s
-                    squares = jnp.sum(s * s, axis=1, keepdims=True)
-                    square_ref[...] = jnp.where(
-                        lane_id == block * tables + t, squares, square_ref[...]
-                    )
-            return carry
-
-        lax.fori_loop(0, tiles, tile_step, 0)
+                    k = 2 * t + h
+                    is_upper = upper_t[:, k * chunks + c : k * chunks + c + 1]
+                    src = slice(c * group + h * group // 2, c * group + (h + 1) * group // 2)
+                    terms = got_ref[t, src].reshape(128, width)
+                    up = jnp.broadcast_to(is_upper, (128, width)).astype(BF16)
+                    row = slice(c * 256 + h * 128, c * 256 + (h + 1) * 128)
+                    rhs_ref[row, width:] = terms * up
+                    rhs_ref[row, :width] = terms * (BF16(1.0) - up)
+            depth = (c1 - c0) * 256
+            span = slice(c0 * 256, c1 * 256)
+
+            def tile_step(m, carry):
+                hot = hot_ref[:, span]
+                mask = jnp.where(hot == m.astype(F32).astype(BF16), BF16(1.0), BF16(0.0))
+                lhs = (low_ref[:, span].reshape(16, 16, depth) * mask[None]).reshape(256, depth)
+                both = jnp.dot(lhs, rhs_ref[span, :], preferred_element_type=F32)
+                for p in range(2):
+                    for h in range(2):
+                        s = both[h * 128 : (h + 1) * 128, p * width : (p + 1) * width]
+                        block = p * (half // 128) + 2 * m + h
+                        at = pl.ds(pl.multiple_of(block * 128, 128), 128)
+                        if c0 > 0:
+                            s = s + sum_ref[at, :]
+                        sum_ref[at, :] = s
+                        if c1 == chunks:
+                            squares = jnp.sum(s * s, axis=1, keepdims=True)
+                            square_ref[...] = jnp.where(
+                                lane_id == block * tables + t, squares, square_ref[...]
+                            )
+                return carry
+
+            lax.fori_loop(0, tiles, tile_step, 0, unroll=2 if depth > 1024 else 4)
+
+        if t < last:
+            wait_for(got_ref.at[t], recv_sem.at[t], 0, peers - 1)
+            add_chunks(0, chunks)
+        else:
+            for (c0, c1), s in zip(tail, tail_sems):
+                wait_for(got_ref.at[t], recv_sem.at[s], c0 * group, min(c1 * group, peers - 1))
+                add_chunks(c0, c1)
         if t == tables - 1:
             part_ref[...] = jnp.broadcast_to(
                 jnp.sum(square_ref[...], axis=0, keepdims=True), part_ref.shape
@@ -306,36 +338,35 @@
                 send_all(
                     lambda p: part_ref.at[pl.ds(0, 1)],
                     lambda slot: parts_ref.at[slot],
-                    tables + 1,
+                    parts_sem,
                 )
     nacc_ref[...] = (acc_t + square_ref[...] * F32(1.0 / width)).T
     parts_ref[pl.ds(peers - 1, 1)] = part_ref[0:1].reshape(1, 1, 128)
-    pltpu.make_async_copy(
-        parts_ref.at[others], parts_ref.at[others], recv_sem.at[tables + 1]
-    ).wait()
+    wait_for(parts_ref, recv_sem.at[parts_sem], 0, peers - 1)
     total = jnp.sum(parts_ref[...].reshape(peers, 128), axis=0, keepdims=True)
     total = jnp.sum(total, axis=1, keepdims=True)
     scale_ref[...] = jnp.broadcast_to(jnp.sqrt(total * F32(1.0 / count)), scale_ref.shape)
+    for t in range(last):
+        wait_for(send_ref.at[t], send_sem.at[t], 0, peers - 1)
+    for (c0, c1), s in zip(tail, tail_sems):
+        wait_for(send_ref.at[last], send_sem.at[s], c0 * group, min(c1 * group, peers - 1))
+    wait_for(srow_ref, send_sem.at[rows_sem], 0, peers - 1)
+    wait_for(parts_ref, send_sem.at[parts_sem], 0, peers - 1)
+
+
+def write_out(tab_ref, acc_ref, scale_ref, out_ref, nacc_ref, total_ref, sem):
+    tables, rows, _ = tab_ref.shape
+    stores = [pltpu.make_async_copy(acc_ref, nacc_ref, sem.at[2 * tables])]
     for t in range(tables):
-        pltpu.make_async_copy(
-            send_ref.at[t, others], send_ref.at[t, others], send_sem.at[t]
-        ).wait()
-    pltpu.make_async_copy(
-        srow_ref.at[others], srow_ref.at[others], send_sem.at[tables]
-    ).wait()
-    pltpu.make_async_copy(
-        parts_ref.at[others], parts_ref.at[others], send_sem.at[tables + 1]
-    ).wait()
-
-
-def write_out(tab_ref, acc_ref, scale_ref, out_ref, nacc_ref, total_ref, sem):
-    tables = tab_ref.shape[0]
-    stores = [
-        pltpu.make_async_copy(tab_ref.at[t], out_ref.at[t], sem.at[t]) for t in range(tables)
-    ]
+        for h in range(2):
+            part = pl.ds(h * rows // 2, rows // 2)
+            stores.append(
+                pltpu.make_async_copy(
+                    tab_ref.at[t, part], out_ref.at[t, part], sem.at[2 * t + h]
+                )
+            )
     for store in stores:
         store.start()
-    nacc_ref[...] = acc_ref[...]
     total_ref[...] = scale_ref[0:1, 0:1]
     for store in stores:
         store.wait()
@@ -355,7 +386,7 @@
     acc = accumulators.reshape(count_tables, blocks, 128).transpose(1, 0, 2).reshape(-1, 128)
     moved, new_acc, scale = pl.pallas_call(
         functools.partial(
-            exchange_and_update, sizes, 37, rows_dev.bit_length() - 1, bucket, count
+            exchange_and_update, sizes, rows_dev.bit_length() - 1, bucket, count
         ),
         out_shape=(
             VMEM(tables.shape, F32),
@@ -384,8 +415,8 @@
             VMEM((8, 128), F32),
             VMEM((peers, 1, 128), F32),
             pltpu.SemaphoreType.DMA((count_tables + 4,)),
-            pltpu.SemaphoreType.DMA((count_tables + 2,)),
-            pltpu.SemaphoreType.DMA((count_tables + 2,)),
+            pltpu.SemaphoreType.DMA((count_tables + 4,)),
+            pltpu.SemaphoreType.DMA((count_tables + 4,)),
         ],
         compiler_params=pltpu.CompilerParams(
             collective_id=0, has_side_effects=True, vmem_limit_bytes=58_585_088
@@ -406,8 +437,8 @@
             jax.ShapeDtypeStruct((1, 1), F32),
         ),
         in_specs=[in_vmem] * 3,
-        out_specs=(in_any, in_vmem, in_vmem),
-        scratch_shapes=[pltpu.SemaphoreType.DMA((count_tables,))],
+        out_specs=(in_any, in_any, in_vmem),
+        scratch_shapes=[pltpu.SemaphoreType.DMA((2 * count_tables + 1,))],
         compiler_params=pltpu.CompilerParams(vmem_limit_bytes=16 * 2**20),
         name="write_out",
     )(moved, new_acc, scale)

time: 55.9 us -> 53.9 us (0.964)
  Pallas kernels: 55 us -> 53 us
    pallas_call x1, Pallas kernels: 51 us -> 49.1 us  [per_device(): pl.pallas_call(functools.partial(exchange_and_update, sizes, rows_dev.bit...]
where the time goes in v2:
time: 53.9 us; the launch traced here: 53.8 us
  Pallas kernels  53 us (98%)
  between operations  0.8 us (1%)
    pallas_call x1, Pallas kernels, per_device(): pl.pallas_call(functools.partial(exchange_and_update, sizes, rows_dev.bit...  49.1 us
    pallas_call x1, Pallas kernels, per_device(): pl.pallas_call(write_out, out_shape=(jax.ShapeDtypeStruct(tables.shape, F...  3.91 us

profile of v2, /device:TPU:1, one launch (start us, length us, event | category | flops | bytes accessed | tf_op | source)
XLA Modules:
  0.0 53.8 jit_solution(13178659188385091437)
XLA Ops:
  0.6 49.1 %exchange.1 = (f32[4,4096,128]{2,1,0:T(8,128)S(1)}, f32[128,128]{1,0:T(8,128)S(1)}, f32[8,128]{1,0:T(8,128)S(1)}) custom-call(s32[4,8,256]{2,1,0:T(8,128)} %bitcast.16, s32[4,256]{1,0:T(4,128)} %bitcast.17, bf16[1024,128]{1,0:T(8,128)(2,1)} %bitcast.14, f32[128,128]{1,0:T(8,128)} %bitcast.15, f32[4,4096,128]{2,1,0:T(8,128)} %tab_ref.1), custom_call_target="tpu_custom_call" | custom-call | tf_op jit(solution)/shard_map/exchange/pallas_call | solution.py:387
  49.8 3.9 %write_out.1 = (f32[4,4096,128]{2,1,0:T(8,128)}, f32[128,128]{1,0:T(8,128)}, f32[1,1]{1,0:T(1,128)}) custom-call(f32[4,4096,128]{2,1,0:T(8,128)S(1)} %get-tuple-element.9.tab_ref, f32[128,128]{1,0:T(8,128)S(1)} %get-tuple-element.10.acc_ref, f32[8,128]{1,0:T(8,128)S(1)} %get-tuple-element.11.scale_ref), custom_call_target="tpu_custom_call" | custom-call | tf_op jit(solution)/shard_map/write_out/pallas_call | solution.py:432

commit v3 on v2

--- a/solution.py
+++ b/solution.py
@@ -26,6 +26,11 @@
 
 def nt_dot(a, b):
     return lax.dot_general(a, b, (((1,), (1,)), ((), ())), preferred_element_type=F32)
+
+
+EVEN = 2
+WIDE = 4
+UNROLL = 1
 
 
 def send_order(sizes):
@@ -189,17 +194,15 @@
         [r for _, r in ranked] + [jnp.zeros((peers, 128 - tables * bucket), I32)], axis=1
     ).reshape(srow_ref.shape)
 
-    def send_all(src, dst, s, slots=range(peers - 1)):
-        for slot in slots:
-            p = peer_at(slot)
-            pltpu.make_async_remote_copy(
-                src_ref=src(p),
-                dst_ref=dst(slot),
-                send_sem=send_sem.at[s],
-                recv_sem=recv_sem.at[s],
-                device_id=(p,),
-                device_id_type=MESH,
-            ).start()
+    def send(p, src, dst, s):
+        pltpu.make_async_remote_copy(
+            src_ref=src,
+            dst_ref=dst,
+            send_sem=send_sem.at[s],
+            recv_sem=recv_sem.at[s],
+            device_id=(p,),
+            device_id_type=MESH,
+        ).start()
 
     last = tables - 1
     rows_sem = tables
@@ -208,17 +211,14 @@
     tail_sems = [last, tables + 2, tables + 3]
 
     def send_table(t):
-        def src(p):
-            return send_ref.at[t, p]
-
-        def dst(slot):
-            return got_ref.at[t, slot]
-
-        if t < last:
-            send_all(src, dst, t, even)
-        else:
-            for (c0, c1), s in zip(tail, tail_sems):
-                send_all(src, dst, s, range(c0 * group, min(c1 * group, peers - 1)))
+        for slot in even if t < EVEN else range(peers - 1):
+            p = peer_at(slot)
+            if t == 0:
+                send(p, srow_ref.at[p], grow_ref.at[slot], rows_sem)
+            sem = t
+            if t == last:
+                sem = next(s for (_, c1), s in zip(tail, tail_sems) if slot < c1 * group)
+            send(p, send_ref.at[t, p], got_ref.at[t, slot], sem)
 
     def wait_for(ref, s, begin, end):
         part = ref.at[pl.ds(begin, end - begin)]
@@ -229,14 +229,15 @@
     select_table(1, ranked[1][0], scaled_ref, send_ref, rows32_ref)
     pl.semaphore_wait(barrier, peers - 1)
     send_table(0)
-    send_all(lambda p: srow_ref.at[p], lambda slot: grow_ref.at[slot], rows_sem, even)
     for t in range(2, tables):
         select_table(t, ranked[t][0], scaled_ref, send_ref, rows32_ref)
-        send_table(t - 1)
+        if t == 2:
+            send_table(1)
     grow_ref[pl.ds(peers - 1, 1)] = srow_ref[pl.ds(me, 1)]
     for t in range(tables):
         got_ref[t, pl.ds(peers - 1, 1)] = send_ref[t, pl.ds(me, 1)]
-    send_table(tables - 1)
+    wait_for(send_ref.at[0], send_sem.at[0], 0, peers - 1)
+    send_table(2)
     acc_t = acc_ref[...].T
     square_ref[...] = jnp.zeros_like(square_ref)
 
@@ -296,17 +297,23 @@
 
             def tile_step(m, carry):
                 hot = hot_ref[:, span]
-                mask = jnp.where(hot == m.astype(F32).astype(BF16), BF16(1.0), BF16(0.0))
-                lhs = (low_ref[:, span].reshape(16, 16, depth) * mask[None]).reshape(256, depth)
-                both = jnp.dot(lhs, rhs_ref[span, :], preferred_element_type=F32)
+                low = low_ref[:, span].reshape(16, 16, depth)
+                lhs = []
+                for i in range(WIDE):
+                    at_tile = hot == (WIDE * m + i).astype(F32).astype(BF16)
+                    mask = jnp.where(at_tile, BF16(1.0), BF16(0.0))
+                    lhs.append((low * mask[None]).reshape(256, depth))
+                both = jnp.dot(
+                    jnp.concatenate(lhs, axis=0), rhs_ref[span, :], preferred_element_type=F32
+                )
                 for p in range(2):
-                    for h in range(2):
+                    for h in range(2 * WIDE):
                         s = both[h * 128 : (h + 1) * 128, p * width : (p + 1) * width]
-                        block = p * (half // 128) + 2 * m + h
+                        block = p * (half // 128) + 2 * WIDE * m + h
                         at = pl.ds(pl.multiple_of(block * 128, 128), 128)
                         if c0 > 0:
-                            s = s + sum_ref[at, :]
-                        sum_ref[at, :] = s
+                            s = s + sum_ref[t, at, :]
+                        sum_ref[t, at, :] = s
                         if c1 == chunks:
                             squares = jnp.sum(s * s, axis=1, keepdims=True)
                             square_ref[...] = jnp.where(
@@ -314,8 +321,11 @@
                             )
                 return carry
 
-            lax.fori_loop(0, tiles, tile_step, 0, unroll=2 if depth > 1024 else 4)
-
+            lax.fori_loop(0, tiles // WIDE, tile_step, 0, unroll=UNROLL if depth > 1024 else 2)
+
+        if t == 1:
+            wait_for(send_ref.at[1], send_sem.at[1], 0, peers - 1)
+            send_table(3)
         if t < last:
             wait_for(got_ref.at[t], recv_sem.at[t], 0, peers - 1)
             add_chunks(0, chunks)
@@ -323,31 +333,26 @@
             for (c0, c1), s in zip(tail, tail_sems):
                 wait_for(got_ref.at[t], recv_sem.at[s], c0 * group, min(c1 * group, peers - 1))
                 add_chunks(c0, c1)
-        if t == tables - 1:
-            part_ref[...] = jnp.broadcast_to(
-                jnp.sum(square_ref[...], axis=0, keepdims=True), part_ref.shape
-            )
-        new_acc = acc_t + square_ref[...] * F32(1.0 / width)
-        rate = STEP / (jnp.sqrt(new_acc) + EPS)
+    part_ref[...] = jnp.broadcast_to(
+        jnp.sum(square_ref[...], axis=0, keepdims=True), part_ref.shape
+    )
+    new_acc = acc_t + square_ref[...] * F32(1.0 / width)
+    rate = STEP / (jnp.sqrt(new_acc) + EPS)
+    nacc_ref[...] = new_acc.T
+    for slot in range(peers - 1):
+        send(peer_at(slot), part_ref.at[pl.ds(0, 1)], parts_ref.at[slot], parts_sem)
+    for t in range(tables):
         loads[t].wait()
         for block in range(rows // 128):
             at = slice(block * 128, (block + 1) * 128)
             lane_at = block * tables + t
-            out_ref[t, at, :] = out_ref[t, at, :] - sum_ref[at, :] * rate[:, lane_at : lane_at + 1]
-            if t == tables - 1 and block == 3:
-                send_all(
-                    lambda p: part_ref.at[pl.ds(0, 1)],
-                    lambda slot: parts_ref.at[slot],
-                    parts_sem,
-                )
-    nacc_ref[...] = (acc_t + square_ref[...] * F32(1.0 / width)).T
+            out_ref[t, at, :] = out_ref[t, at, :] - sum_ref[t, at, :] * rate[:, lane_at : lane_at + 1]
     parts_ref[pl.ds(peers - 1, 1)] = part_ref[0:1].reshape(1, 1, 128)
     wait_for(parts_ref, recv_sem.at[parts_sem], 0, peers - 1)
     total = jnp.sum(parts_ref[...].reshape(peers, 128), axis=0, keepdims=True)
     total = jnp.sum(total, axis=1, keepdims=True)
     scale_ref[...] = jnp.broadcast_to(jnp.sqrt(total * F32(1.0 / count)), scale_ref.shape)
-    for t in range(last):
-        wait_for(send_ref.at[t], send_sem.at[t], 0, peers - 1)
+    wait_for(send_ref.at[2], send_sem.at[2], 0, peers - 1)
     for (c0, c1), s in zip(tail, tail_sems):
         wait_for(send_ref.at[last], send_sem.at[s], c0 * group, min(c1 * group, peers - 1))
     wait_for(srow_ref, send_sem.at[rows_sem], 0, peers - 1)
@@ -407,7 +412,7 @@
             VMEM((samples * count_tables, width), F32),
             VMEM((count_tables, samples, width), BF16),
             VMEM((peers * bucket, width), F32),
-            VMEM((rows_dev, width), F32),
+            VMEM(tables.shape, F32),
             VMEM((256, lookups), BF16),
             VMEM((16, lookups), BF16),
             VMEM((lookups, 2 * width), BF16),

time: 53.9 us -> 51.4 us (0.954)
  Pallas kernels: 53 us -> 50.5 us
    pallas_call x1, Pallas kernels: 49.1 us -> 46.6 us  [per_device(): pl.pallas_call(functools.partial(exchange_and_update, sizes, rows_dev.bit...]
where the time goes in v3:
time: 51.4 us; the launch traced here: 51.3 us
  Pallas kernels  50.5 us (98%)
  between operations  0.8 us (2%)
    pallas_call x1, Pallas kernels, per_device(): pl.pallas_call(functools.partial(exchange_and_update, sizes, rows_dev.bit...  46.6 us
    pallas_call x1, Pallas kernels, per_device(): pl.pallas_call(write_out, out_shape=(jax.ShapeDtypeStruct(tables.shape, F...  3.91 us

profile of v3, /device:TPU:1, one launch (start us, length us, event | category | flops | bytes accessed | tf_op | source)
XLA Modules:
  0.0 51.3 jit_solution(12520206134394724995)
XLA Ops:
  0.6 46.6 %exchange.1 = (f32[4,4096,128]{2,1,0:T(8,128)S(1)}, f32[128,128]{1,0:T(8,128)S(1)}, f32[8,128]{1,0:T(8,128)S(1)}) custom-call(s32[4,8,256]{2,1,0:T(8,128)} %bitcast.16, s32[4,256]{1,0:T(4,128)} %bitcast.17, bf16[1024,128]{1,0:T(8,128)(2,1)} %bitcast.14, f32[128,128]{1,0:T(8,128)} %bitcast.15, f32[4,4096,128]{2,1,0:T(8,128)} %tab_ref.1), custom_call_target="tpu_custom_call" | custom-call | tf_op jit(solution)/shard_map/exchange/pallas_call | solution.py:392
  47.3 3.9 %write_out.1 = (f32[4,4096,128]{2,1,0:T(8,128)}, f32[128,128]{1,0:T(8,128)}, f32[1,1]{1,0:T(1,128)}) custom-call(f32[4,4096,128]{2,1,0:T(8,128)S(1)} %get-tuple-element.9.tab_ref, f32[128,128]{1,0:T(8,128)S(1)} %get-tuple-element.10.acc_ref, f32[8,128]{1,0:T(8,128)S(1)} %get-tuple-element.11.scale_ref), custom_call_target="tpu_custom_call" | custom-call | tf_op jit(solution)/shard_map/write_out/pallas_call | solution.py:437

commit v4 on v3

--- a/solution.py
+++ b/solution.py
@@ -39,7 +39,7 @@
         peers *= size
     even = []
     for k in range(peers - 1):
-        rest = (37 * k) % (peers - 1) + 1
+        rest = (29 * k) % (peers - 1) + 1
         offset = []
         for size in reversed(sizes):
             offset.insert(0, rest % size)
@@ -207,8 +207,8 @@
     last = tables - 1
     rows_sem = tables
     parts_sem = tables + 1
-    tail = [(0, chunks // 2), (chunks // 2, 3 * chunks // 4), (3 * chunks // 4, chunks)]
-    tail_sems = [last, tables + 2, tables + 3]
+    tail = [(0, chunks // 2), (chunks // 2, chunks)]
+    tail_sems = [last, tables + 2]
 
     def send_table(t):
         for slot in even if t < EVEN else range(peers - 1):
@@ -420,8 +420,8 @@
             VMEM((8, 128), F32),
             VMEM((peers, 1, 128), F32),
             pltpu.SemaphoreType.DMA((count_tables + 4,)),
-            pltpu.SemaphoreType.DMA((count_tables + 4,)),
-            pltpu.SemaphoreType.DMA((count_tables + 4,)),
+            pltpu.SemaphoreType.DMA((count_tables + 3,)),
+            pltpu.SemaphoreType.DMA((count_tables + 3,)),
         ],
         compiler_params=pltpu.CompilerParams(
             collective_id=0, has_side_effects=True, vmem_limit_bytes=58_585_088

time: 51.4 us -> 51.3 us (level)
  no operation moved by 1% of the time
where the time goes in v4:
time: 51.3 us; the launch traced here: 51.2 us
  Pallas kernels  50.4 us (98%)
  between operations  0.8 us (2%)
    pallas_call x1, Pallas kernels, per_device(): pl.pallas_call(functools.partial(exchange_and_update, sizes, rows_dev.bit...  46.5 us
    pallas_call x1, Pallas kernels, per_device(): pl.pallas_call(write_out, out_shape=(jax.ShapeDtypeStruct(tables.shape, F...  3.91 us

profile of v4, /device:TPU:1, one launch (start us, length us, event | category | flops | bytes accessed | tf_op | source)
XLA Modules:
  0.0 51.2 jit_solution(8117075767370353172)
XLA Ops:
  0.6 46.5 %exchange.1 = (f32[4,4096,128]{2,1,0:T(8,128)S(1)}, f32[128,128]{1,0:T(8,128)S(1)}, f32[8,128]{1,0:T(8,128)S(1)}) custom-call(s32[4,8,256]{2,1,0:T(8,128)} %bitcast.16, s32[4,256]{1,0:T(4,128)} %bitcast.17, bf16[1024,128]{1,0:T(8,128)(2,1)} %bitcast.14, f32[128,128]{1,0:T(8,128)} %bitcast.15, f32[4,4096,128]{2,1,0:T(8,128)} %tab_ref.1), custom_call_target="tpu_custom_call" | custom-call | tf_op jit(solution)/shard_map/exchange/pallas_call | solution.py:392
  47.2 3.9 %write_out.1 = (f32[4,4096,128]{2,1,0:T(8,128)}, f32[128,128]{1,0:T(8,128)}, f32[1,1]{1,0:T(1,128)}) custom-call(f32[4,4096,128]{2,1,0:T(8,128)S(1)} %get-tuple-element.9.tab_ref, f32[128,128]{1,0:T(8,128)S(1)} %get-tuple-element.10.acc_ref, f32[8,128]{1,0:T(8,128)S(1)} %get-tuple-element.11.scale_ref), custom_call_target="tpu_custom_call" | custom-call | tf_op jit(solution)/shard_map/write_out/pallas_call | solution.py:437

commit v5 on v4

--- a/solution.py
+++ b/solution.py
@@ -338,9 +338,9 @@
     )
     new_acc = acc_t + square_ref[...] * F32(1.0 / width)
     rate = STEP / (jnp.sqrt(new_acc) + EPS)
-    nacc_ref[...] = new_acc.T
     for slot in range(peers - 1):
         send(peer_at(slot), part_ref.at[pl.ds(0, 1)], parts_ref.at[slot], parts_sem)
+    nacc_ref[...] = new_acc.T
     for t in range(tables):
         loads[t].wait()
         for block in range(rows // 128):

time: 51.3 us -> 51.3 us (level)
  no operation moved by 1% of the time
where the time goes in v5:
time: 51.3 us; the launch traced here: 51.2 us
  Pallas kernels  50.4 us (98%)
  between operations  0.8 us (2%)
    pallas_call x1, Pallas kernels, per_device(): pl.pallas_call(functools.partial(exchange_and_update, sizes, rows_dev.bit...  46.5 us
    pallas_call x1, Pallas kernels, per_device(): pl.pallas_call(write_out, out_shape=(jax.ShapeDtypeStruct(tables.shape, F...  3.91 us

profile of v5, /device:TPU:1, one launch (start us, length us, event | category | flops | bytes accessed | tf_op | source)
XLA Modules:
  0.0 51.2 jit_solution(2197709692896092460)
XLA Ops:
  0.6 46.5 %exchange.1 = (f32[4,4096,128]{2,1,0:T(8,128)S(1)}, f32[128,128]{1,0:T(8,128)S(1)}, f32[8,128]{1,0:T(8,128)S(1)}) custom-call(s32[4,8,256]{2,1,0:T(8,128)} %bitcast.16, s32[4,256]{1,0:T(4,128)} %bitcast.17, bf16[1024,128]{1,0:T(8,128)(2,1)} %bitcast.14, f32[128,128]{1,0:T(8,128)} %bitcast.15, f32[4,4096,128]{2,1,0:T(8,128)} %tab_ref.1), custom_call_target="tpu_custom_call" | custom-call | tf_op jit(solution)/shard_map/exchange/pallas_call | solution.py:392
  47.1 3.9 %write_out.1 = (f32[4,4096,128]{2,1,0:T(8,128)}, f32[128,128]{1,0:T(8,128)}, f32[1,1]{1,0:T(1,128)}) custom-call(f32[4,4096,128]{2,1,0:T(8,128)S(1)} %get-tuple-element.9.tab_ref, f32[128,128]{1,0:T(8,128)S(1)} %get-tuple-element.10.acc_ref, f32[8,128]{1,0:T(8,128)S(1)} %get-tuple-element.11.scale_ref), custom_call_target="tpu_custom_call" | custom-call | tf_op jit(solution)/shard_map/write_out/pallas_call | solution.py:437
